TPU v7x, 256 devices: a whole 4x4x8 slice. The times are simulated.
256 devices in a mesh: owner: 8 (over y, core), rows: 32 (over z, x).
Axes of the slice: x: 4, y: 4, z: 8, core: 2. Of those that a mesh axis runs over, the one named last changes fastest.
Arguments:
- w_gate: float32 [128, 2048, 768], P('owner', 'rows'), may hold values from -0.125 to 0.125
- w_up: float32 [128, 2048, 768], P('owner', 'rows'), may hold values from -0.125 to 0.125
- router_weight: float32 [2048, 128], P('rows', 'owner'), may hold values from -0.125 to 0.125
- router_gain: float32 [2048], P('rows'), may hold values from 0.25 to 1.75
Outputs:
- serve_gate: bfloat16 [128, 768, 2048], P('owner', 'rows')
- serve_up: bfloat16 [128, 768, 2048], P('owner', 'rows')
- serve_router: bfloat16 [2048, 128], replicated
All inputs are finite; a program needn't handle non-finite values.
Results may differ from a plain program's by a relative error of at most 0.001.
Values may be sent and summed in bfloat16 or wider, within the bound.
A program may use at most 64 MiB of HBM per device.

v0:
```python
import jax
import jax.numpy as jnp
from jax import lax
from jax.sharding import Mesh
from jax.sharding import PartitionSpec as P

OWNER = ("owner_0", "owner_1")


def in_order(blocks, dim):
    lengths = list(blocks.shape[1:])
    lengths[dim] *= blocks.shape[0]
    return jnp.moveaxis(blocks, 0, dim).reshape(lengths)


def from_everyone(value, axis):
    copies = jnp.broadcast_to(value, (lax.axis_size(axis), *value.shape))
    return lax.all_to_all(copies, axis, split_axis=0, concat_axis=0, tiled=True)


def gathered_copies(value, axis, dim):
    return in_order(from_everyone(value, axis), dim)


def edges_of(length, count):
    step = length // count
    if step >= 8:
        step -= step % 8
    return [step * k for k in range(1, count)]


def gather_in_order(value, axes, order):
    blocks = value
    for k in order:
        blocks = lax.all_gather(blocks, axes[k])
    done = order[::-1]
    back = [done.index(k) for k in range(len(axes))]
    blocks = blocks.transpose(*back, *range(len(axes), blocks.ndim))
    return blocks.reshape(-1, *value.shape)


def gather_at_once(value, axes, dim):
    split_at = max(range(max(1, value.ndim - 1)), key=lambda d: value.shape[d])
    count, outs = (len(axes), [])
    for initial, slab in enumerate(
        jnp.split(value, edges_of(value.shape[split_at], count), axis=split_at)
    ):
        if slab.size:
            order = [(initial - k) % count for k in range(count)]
            outs.append(gather_in_order(slab, axes, order))
    return in_order(jnp.concatenate(outs, axis=split_at + 1), dim)


def body(w_gate, w_up, router_weight, router_gain):
    narrow_gate, narrow_up = (w_gate.astype(jnp.bfloat16), w_up.astype(jnp.bfloat16))
    serve_gate, serve_up = (
        lax.all_to_all(narrow_gate, "rows", split_axis=2, concat_axis=1, tiled=True),
        lax.all_to_all(narrow_up, "rows", split_axis=2, concat_axis=1, tiled=True),
    )
    serve_gate = jnp.transpose(serve_gate, (0, 2, 1))
    serve_up = jnp.transpose(serve_up, (0, 2, 1))
    part_router = (router_weight * router_gain[:, None]).astype(jnp.bfloat16)
    row_router = gathered_copies(part_router, "rows", 0)
    serve_router = gather_at_once(row_router, OWNER, 1)
    return (serve_gate, serve_up, serve_router)


def solution(mesh):
    torus = Mesh(mesh.devices.reshape(4, 2, mesh.shape["rows"]), ("owner_0", "owner_1", "rows"))
    return jax.shard_map(
        body,
        mesh=torus,
        in_specs=(P(OWNER, "rows", None), P(OWNER, "rows", None), P("rows", OWNER), P("rows")),
        out_specs=(P(OWNER, "rows", None), P(OWNER, "rows", None), P()),
        check_vma=False,
    )
```

profile of v0, /device:TPU:6, one launch (start us, length us, event | category | flops | bytes accessed | tf_op | source)
XLA Modules:
  0.0 137.8 jit_solution(7282913358461512355)
XLA Ops:
  0.6 0.7 multiply_convert_fusion
  1.4 0.8 reshape.31
  2.1 11.6 %all-to-all-start.2 = ((bf16[32,2,512]{2,1,0:T(2,128)(2,1)}), bf16[32,2,512]{2,1,0:T(2,128)(2,1)S(1)}, u32[]{:S(2)}, u32[]{:S(2)}) async-start(bf16[32,2,512]{2,1,0:T(2,128)(2,1)} %reshape.31), calls=%async_computation.2 | async-start | bytes 131072 | tf_op jit(solution)/shard_map/all_to_all | solution.py:18
  13.7 3.2 %convert_element_type.9 = bf16[16,64,768]{2,1,0:T(8,128)(2,1)} convert(f32[16,64,768]{2,1,0:T(8,128)} %param.4) | non-fusion elementwise | flops 786432 | bytes 4718592 | tf_op jit(solution)/shard_map/convert_element_type | solution.py:55
  16.9 4.0 %copy.38 = bf16[16,64,768]{1,0,2:T(8,128)(2,1)S(1)} copy(bf16[16,64,768]{2,1,0:T(8,128)(2,1)} %convert_element_type.9) | data formatting | bytes 3145728 | tf_op jit(solution)/shard_map/convert_element_type | solution.py:55
  20.9 3.2 %reshape.27 = bf16[32,2,12288]{2,1,0:T(2,128)(2,1)} reshape(bf16[768,16,64]{2,1,0:T(8,128)(2,1)S(1)} %bitcast.34) | data formatting | bytes 3145728
  24.1 0.0 copy-start
  24.1 0.0 all-to-all-done.2
  24.1 10.1 %all-to-all-start = ((bf16[32,2,12288]{2,1,0:T(2,128)(2,1)}), bf16[32,2,12288]{2,1,0:T(2,128)(2,1)}, u32[]{:S(2)}, u32[]{:S(2)}) async-start(bf16[32,2,12288]{2,1,0:T(2,128)(2,1)} %reshape.27), calls=%async_computation | async-start | bytes 3145728 | tf_op jit(solution)/shard_map/all_to_all | solution.py:57
  34.2 0.0 copy-done
  34.2 1.3 convert_element_type.10
  35.6 4.0 %copy.41 = bf16[16,64,768]{1,0,2:T(8,128)(2,1)S(1)} copy(bf16[16,64,768]{2,1,0:T(8,128)(2,1)} %convert_element_type.10) | data formatting | bytes 3145728 | tf_op jit(solution)/shard_map/convert_element_type | solution.py:55
  39.6 3.2 %reshape.29 = bf16[32,2,12288]{2,1,0:T(2,128)(2,1)} reshape(bf16[768,16,64]{2,1,0:T(8,128)(2,1)S(1)} %bitcast.35) | data formatting | bytes 3145728
  42.8 30.2 %all-to-all-done = bf16[32,2,12288]{2,1,0:T(2,128)(2,1)} async-done(((bf16[32,2,12288]{2,1,0:T(2,128)(2,1)}), bf16[32,2,12288]{2,1,0:T(2,128)(2,1)}, u32[]{:S(2)}, u32[]{:S(2)}) %all-to-all-start) | async-done | bytes 1572896 | tf_op jit(solution)/shard_map/all_to_all | solution.py:57
  73.0 5.6 %all-to-all-start.1 = ((bf16[32,2,12288]{2,1,0:T(2,128)(2,1)}), bf16[32,2,12288]{2,1,0:T(2,128)(2,1)}, u32[]{:S(2)}, u32[]{:S(2)}) async-start(bf16[32,2,12288]{2,1,0:T(2,128)(2,1)} %reshape.29), calls=%async_computation.1 | async-start | bytes 3145728 | tf_op jit(solution)/shard_map/all_to_all | solution.py:58
  78.6 0.1 reshape.32
  78.8 0.1 all_gather.28
  79.0 0.1 all_gather.24
  79.1 12.7 %all_gather.25 = bf16[4,1024,16]{1,2,0:T(8,128)(2,1)S(1)} all-gather(bf16[1,1024,16]{1,2,0:T(8,128)(2,1)S(1)} %all_gather.24), channel_id=1, replica_groups=mesh['owner_0'=4,'owner_1'=2,'rows'=32] {'owner_0'}, dimensions={0}, use_global_device_ids=true | all-gather | bytes 163840 | tf_op jit(solution)/shard_map/all_gather | solution.py:35
  91.8 2.0 %all-gather = bf16[8,1024,16]{1,2,0:T(8,128)(2,1)S(1)} all-gather(bf16[4,1024,16]{1,2,0:T(8,128)(2,1)S(1)} %all_gather.25), channel_id=2, replica_groups=mesh['owner_0'=4,'owner_1'=2,'rows'=32] {'owner_1'}, dimensions={0}, use_global_device_ids=true | all-gather | bytes 393216 | tf_op jit(solution)/shard_map/all_gather | solution.py:35
  93.8 1.9 %all_gather.29 = bf16[2,1024,16]{1,2,0:T(8,128)(2,1)S(1)} all-gather(bf16[1,1024,16]{1,2,0:T(8,128)(2,1)S(1)} %all_gather.28), channel_id=1, replica_groups=mesh['owner_0'=4,'owner_1'=2,'rows'=32] {'owner_1'}, dimensions={0}, use_global_device_ids=true | all-gather | bytes 98304 | tf_op jit(solution)/shard_map/all_gather | solution.py:35
  95.6 12.4 %all-gather.1 = bf16[8,1024,16]{1,2,0:T(8,128)(2,1)S(1)} all-gather(bf16[2,1024,16]{1,2,0:T(8,128)(2,1)S(1)} %all_gather.29), channel_id=3, replica_groups=mesh['owner_0'=4,'owner_1'=2,'rows'=32] {'owner_0'}, dimensions={0}, use_global_device_ids=true | all-gather | bytes 327680 | tf_op jit(solution)/shard_map/all_gather | solution.py:35
  108.1 1.0 copy.47
  109.1 5.1 %reshape.28 = bf16[768,16,64]{2,1,0:T(8,128)(2,1)S(1)} reshape(bf16[32,2,12288]{2,1,0:T(2,128)(2,1)} %all-to-all-done) | data formatting | bytes 3145728
  114.2 3.7 %copy.40 = bf16[16,32,64,24]{2,1,3,0:T(8,128)(2,1)} copy(bf16[16,32,64,24]{2,0,3,1:T(8,128)(2,1)S(1)} %bitcast.36) | data formatting | bytes 3145728 | tf_op jit(solution)/shard_map/all_to_all | solution.py:57
  117.9 5.6 %all_to_all.32 = bf16[16,2048,24]{1,2,0:T(8,128)(2,1)} reshape(bf16[16,32,64,24]{2,1,3,0:T(8,128)(2,1)} %copy.40) | data formatting | bytes 3145728 | tf_op jit(solution)/shard_map/all_to_all | solution.py:57
  123.5 0.0 all-to-all-done.1
  123.5 5.1 %reshape.30 = bf16[768,16,64]{2,1,0:T(8,128)(2,1)S(1)} reshape(bf16[32,2,12288]{2,1,0:T(2,128)(2,1)} %all-to-all-done.1) | data formatting | bytes 3145728
  128.6 3.7 %copy.43 = bf16[16,32,64,24]{2,1,3,0:T(8,128)(2,1)} copy(bf16[16,32,64,24]{2,0,3,1:T(8,128)(2,1)S(1)} %bitcast.37) | data formatting | bytes 3145728 | tf_op jit(solution)/shard_map/all_to_all | solution.py:58
  132.2 5.6 %all_to_all.36 = bf16[16,2048,24]{1,2,0:T(8,128)(2,1)} reshape(bf16[16,32,64,24]{2,1,3,0:T(8,128)(2,1)} %copy.43) | data formatting | bytes 3145728 | tf_op jit(solution)/shard_map/all_to_all | solution.py:58
  (6 shorter events, 0.1 us)
Async XLA Ops:
  2.1 22.0 %all-to-all-start.2 = ((bf16[32,2,512]{2,1,0:T(2,128)(2,1)}), bf16[32,2,512]{2,1,0:T(2,128)(2,1)S(1)}, u32[]{:S(2)}, u32[]{:S(2)}) async-start(bf16[32,2,512]{2,1,0:T(2,128)(2,1)} %reshape.31), calls=%async_computation.2 | async-start | bytes 131072 | tf_op jit(solution)/shard_map/all_to_all | solution.py:18
  24.1 10.1 %copy-start = (f32[16,64,768]{2,1,0:T(8,128)S(1)}, f32[16,64,768]{2,1,0:T(8,128)}, u32[]{:S(2)}) copy-start(f32[16,64,768]{2,1,0:T(8,128)} %param.5) | copy-start | bytes 9437188
  24.1 48.9 %all-to-all-start = ((bf16[32,2,12288]{2,1,0:T(2,128)(2,1)}), bf16[32,2,12288]{2,1,0:T(2,128)(2,1)}, u32[]{:S(2)}, u32[]{:S(2)}) async-start(bf16[32,2,12288]{2,1,0:T(2,128)(2,1)} %reshape.27), calls=%async_computation | async-start | bytes 3145728 | tf_op jit(solution)/shard_map/all_to_all | solution.py:57
  73.0 50.4 %all-to-all-start.1 = ((bf16[32,2,12288]{2,1,0:T(2,128)(2,1)}), bf16[32,2,12288]{2,1,0:T(2,128)(2,1)}, u32[]{:S(2)}, u32[]{:S(2)}) async-start(bf16[32,2,12288]{2,1,0:T(2,128)(2,1)} %reshape.29), calls=%async_computation.1 | async-start | bytes 3145728 | tf_op jit(solution)/shard_map/all_to_all | solution.py:58
where the time goes:
time: 139 us; the launch traced here: 138 us
  local copies, waits for them, and re-layouts  45.3 us (33%)
  waiting for transfers between devices  30.2 us (22%)
  blocking collectives  28.9 us (21%)
  starting transfers between devices  27.3 us (20%)
  other arithmetic  5.31 us (4%)
    all_to_all x1, waiting for transfers between devices, body(): lax.all_to_all(narrow_gate, 'rows', split_axis=2, concat_axis=1, tiled=True)  30.2 us
    all_gather x4, blocking collectives, gather_in_order(): blocks = lax.all_gather(blocks, axes[k])  28.9 us
    unnamed x10, local copies, waits for them, and re-layouts  18.5 us
    all_to_all x1, starting transfers between devices, from_everyone(): return lax.all_to_all(copies, axis, split_axis=0, concat_axis=0, tiled=True)  11.6 us
    all_to_all x1, starting transfers between devices, body(): lax.all_to_all(narrow_gate, 'rows', split_axis=2, concat_axis=1, tiled=True)  10.1 us
    all_to_all x2, local copies, waits for them, and re-layouts, body(): lax.all_to_all(narrow_gate, 'rows', split_axis=2, concat_axis=1, tiled=True)  9.25 us
    all_to_all x2, local copies, waits for them, and re-layouts, body(): lax.all_to_all(narrow_up, 'rows', split_axis=2, concat_axis=1, tiled=True)  9.25 us
    all_to_all x1, starting transfers between devices, body(): lax.all_to_all(narrow_up, 'rows', split_axis=2, concat_axis=1, tiled=True)  5.61 us
  transfers between devices with their start and end apart: 3, of which 1 were waited for; matrix products, arithmetic and copies ran while one was open for 21% of the time, Pallas kernels for 0%

commit v1 on v0

v1 whole, which is shorter than its diff:
```python
import jax
import jax.numpy as jnp
from jax import lax
from jax.experimental import pallas as pl
from jax.experimental.pallas import tpu as pltpu
from jax.sharding import PartitionSpec as P

MESH = pl.DeviceIdType.MESH
NZ, NX, NY, CORES = 8, 4, 4, 2
ROWS = NZ * NX
LANES, SUB = 128, 8


def place():
    owner, rows = lax.axis_index("owner"), lax.axis_index("rows")
    return owner // CORES, lax.rem(owner, CORES), rows // NX, lax.rem(rows, NX)


def beside(value, step, count):
    return lax.rem(value + step, count)


def rows_of(k):
    _, _, z, x = place()
    return beside(z, k // NX, NZ) * NX + beside(x, lax.rem(k, NX), NX)


def merged(even, odd):
    low = lax.broadcasted_iota(jnp.int32, even.shape, even.ndim - 1) < LANES // 2
    turned_odd = pltpu.roll(odd, LANES // 2, odd.ndim - 1)
    turned_even = pltpu.roll(even, LANES // 2, even.ndim - 1)
    return jnp.where(low, even, turned_odd), jnp.where(low, turned_even, odd)


def kernel(
    gate, up, weight, gain, out_gate, out_up, out_router,
    staged, send, recv, pieces, in_sem, send_sem, recv_sem, piece_send, piece_recv,
):
    y, core, z, x = place()
    owner, rows = lax.axis_index("owner"), lax.axis_index("rows")
    pairs = gate.shape[0]
    width = gate.shape[2]
    tiles = width // ROWS // SUB
    sources = (gate, up)

    def load(a, p):
        return pltpu.make_async_copy(sources[a].at[p], staged.at[p, a], in_sem.at[p, a])

    def load_all(p, _):
        for a in range(2):
            load(a, p).start()
        return 0

    lax.fori_loop(0, pairs, load_all, 0)

    barrier = pltpu.get_barrier_semaphore()

    def greet(k, _):
        pl.semaphore_signal(barrier, inc=1, device_id={"rows": rows_of(k)}, device_id_type=MESH)
        return 0

    lax.fori_loop(1, ROWS, greet, 0)
    y_peers = [beside(y, k, NY) * CORES + core for k in range(1, NY)]
    partner = y * CORES + (1 - core)
    for peer in (*y_peers, partner):
        pl.semaphore_signal(barrier, inc=1, device_id={"owner": peer}, device_id_type=MESH)

    scaled = weight[...] * gain[...]
    pieces[core, y, x, z] = jnp.concatenate([scaled[:SUB], scaled[SUB:]], axis=1).astype(jnp.bfloat16)

    def prepare(p):
        for a in range(2):
            load(a, p).wait()
            for k in range(width // LANES):
                block = staged[p, a, :, k * LANES : (k + 1) * LANES].T.reshape(LANES // SUB, SUB, LANES)
                block = block.astype(jnp.bfloat16)
                for i in range(LANES // SUB):
                    g = k * (LANES // SUB) + i
                    send[p, g // tiles, a * tiles + g % tiles] = block[i]
        recv[p, rows] = send[p, rows]

    def move(p, peer):
        return pltpu.make_async_remote_copy(
            send.at[p, peer], recv.at[p, rows], send_sem.at[p], recv_sem.at[p, rows],
            device_id={"rows": peer}, device_id_type=MESH,
        )

    def send_all(p):
        def one(k, _):
            move(p, rows_of(k)).start()
            return 0

        lax.fori_loop(1, ROWS, one, 0)

    def arrived(p, source):
        pltpu.make_async_remote_copy(
            send.at[p, source], recv.at[p, source], send_sem.at[p], recv_sem.at[p, source],
            device_id={"rows": rows}, device_id_type=MESH,
        ).wait_recv()

    def assemble(p):
        def pair(j, _):
            for s in (2 * j, 2 * j + 1):
                @pl.when(s != rows)
                def _():
                    arrived(p, s)

            low, high = merged(recv[p, 2 * j], recv[p, 2 * j + 1])
            lanes = pl.ds(pl.multiple_of(j * LANES, LANES), LANES)
            for a, out in enumerate((out_gate, out_up)):
                out[2 * p, :, :, lanes] = low[a * tiles : (a + 1) * tiles]
                out[2 * p + 1, :, :, lanes] = high[a * tiles : (a + 1) * tiles]
            return 0

        lax.fori_loop(0, ROWS // 2, pair, 0)

    def to_z(k):
        mine = pieces.at[core, y, x, z]
        return pltpu.make_async_remote_copy(
            mine, mine, piece_send.at[0, k], piece_recv.at[0, k],
            device_id={"rows": beside(z, k, NZ) * NX + x}, device_id_type=MESH,
        )

    def to_x(k):
        mine = pieces.at[core, y, x]
        return pltpu.make_async_remote_copy(
            mine, mine, piece_send.at[1, k], piece_recv.at[1, k],
            device_id={"rows": z * NX + beside(x, k, NX)}, device_id_type=MESH,
        )

    def to_y(k):
        mine = pieces.at[core, y]
        return pltpu.make_async_remote_copy(
            mine, mine, piece_send.at[2, k], piece_recv.at[2, k],
            device_id={"owner": beside(y, k, NY) * CORES + core}, device_id_type=MESH,
        )

    def to_core(k):
        mine = pieces.at[core]
        return pltpu.make_async_remote_copy(
            mine, mine, piece_send.at[3, k], piece_recv.at[3, k],
            device_id={"owner": partner}, device_id_type=MESH,
        )

    stages = ((to_z, NZ), (to_x, NX), (to_y, NY), (to_core, CORES))

    def begin(stage):
        to, count = stages[stage]
        for k in range(1, count):
            to(k).start()

    def end(stage):
        to, count = stages[stage]
        for k in range(1, count):
            to(k).wait()

    def router():
        for zz in range(NZ):
            for half in range(NX // 2):
                blocks = []
                for o in range(NY * CORES):
                    low, high = merged(
                        pieces[o % CORES, o // CORES, 2 * half, zz], pieces[o % CORES, o // CORES, 2 * half + 1, zz]
                    )
                    blocks += [low, high]
                block = jnp.concatenate([b.astype(jnp.float32) for b in blocks], axis=0)
                at = (zz * NX + 2 * half) * LANES // 2
                out_router[at : at + LANES, :] = block.T.astype(jnp.bfloat16)

    prepare(0)
    pl.semaphore_wait(barrier, ROWS - 1 + NY)
    begin(0)
    send_all(0)
    prepare(1)
    send_all(1)
    end(0)
    begin(1)
    for p in (2, 3):
        prepare(p)
        send_all(p)
    end(1)
    begin(2)

    def rest(p, _):
        prepare(p)
        send_all(p)
        return 0

    lax.fori_loop(4, pairs, rest, 0)
    assemble(0)
    end(2)
    begin(3)
    assemble(1)
    end(3)
    router()

    def finish(p, _):
        assemble(p)
        return 0

    lax.fori_loop(2, pairs, finish, 0)

    def sent(p, _):
        others = pl.ds(0, ROWS - 1)
        pltpu.make_async_remote_copy(
            send.at[p, others], recv.at[p, others], send_sem.at[p], recv_sem.at[p, 0],
            device_id={"rows": rows}, device_id_type=MESH,
        ).wait_send()
        return 0

    lax.fori_loop(0, pairs, sent, 0)


def body(w_gate, w_up, router_weight, router_gain):
    experts, share, width = w_gate.shape
    pairs, model = experts // 2, share * ROWS
    tiles = width // ROWS // SUB
    paired = (pairs, 2 * share, width)
    vmem, anywhere = pl.BlockSpec(memory_space=pltpu.VMEM), pl.BlockSpec(memory_space=pl.ANY)
    gate, up, router = pl.pallas_call(
        kernel,
        out_shape=(
            jax.ShapeDtypeStruct((experts, tiles, SUB, model), jnp.bfloat16),
            jax.ShapeDtypeStruct((experts, tiles, SUB, model), jnp.bfloat16),
            jax.ShapeDtypeStruct((model, experts * NY * CORES), jnp.bfloat16),
        ),
        in_specs=[anywhere, anywhere, vmem, vmem],
        out_specs=(vmem, vmem, vmem),
        scratch_shapes=[
            pltpu.VMEM((pairs, 2, 2 * share, width), jnp.float32),
            pltpu.VMEM((pairs, ROWS, 2 * tiles, SUB, LANES), jnp.bfloat16),
            pltpu.VMEM((pairs, ROWS, 2 * tiles, SUB, LANES), jnp.bfloat16),
            pltpu.VMEM((CORES, NY, NX, NZ, SUB, LANES), jnp.bfloat16),
            pltpu.SemaphoreType.DMA((pairs, 2)),
            pltpu.SemaphoreType.DMA((pairs,)),
            pltpu.SemaphoreType.DMA((pairs, ROWS)),
            pltpu.SemaphoreType.DMA((4, NZ)),
            pltpu.SemaphoreType.DMA((4, NZ)),
        ],
        compiler_params=pltpu.CompilerParams(collective_id=0, has_side_effects=True, vmem_limit_bytes=50000000),
        name="serve",
    )(w_gate.reshape(paired), w_up.reshape(paired), router_weight.T, router_gain.reshape(1, share))
    shape = (experts, tiles * SUB, model)
    return gate.reshape(shape), up.reshape(shape), router


def solution(mesh):
    return jax.shard_map(
        body,
        mesh=mesh,
        in_specs=(P("owner", "rows", None), P("owner", "rows", None), P("rows", "owner"), P("rows")),
        out_specs=(P("owner", "rows", None), P("owner", "rows", None), P()),
        check_vma=False,
    )
```

time: 139 us -> 89.3 us (0.64)
  Pallas kernels: 0 us -> 83.4 us
  local copies, waits for them, and re-layouts: 45.3 us -> 4.42 us
  waiting for transfers between devices: 30.2 us -> 0 us
  blocking collectives: 28.9 us -> 0 us
  starting transfers between devices: 27.3 us -> 0 us
  other arithmetic: 5.31 us -> 0 us
    pallas_call x0 -> x1, Pallas kernels: none -> 83.4 us  [body(): pl.pallas_call(kernel, out_shape=(jax.ShapeDtypeStruct((experts, tiles, S...]
    all_to_all x3 -> x0, waiting for transfers between devices: 30.2 us -> none  [the longest x1 30.2 us: body(): lax.all_to_all(narrow_gate, 'rows', split_axis=2, concat_axis=1, tiled=True)]
    all_gather x4 -> x0, blocking collectives: 28.9 us -> none  [gather_in_order(): blocks = lax.all_gather(blocks, axes[k])]
    all_to_all x3 -> x0, starting transfers between devices: 27.3 us -> none  [the longest x1 11.6 us: from_everyone(): return lax.all_to_all(copies, axis, split_axis=0, concat_axis=0, tiled=True)]
    all_to_all x4 -> x0, local copies, waits for them, and re-layouts: 18.5 us -> none  [the longest x2 9.25 us: body(): lax.all_to_all(narrow_gate, 'rows', split_axis=2, concat_axis=1, tiled=True)]
    unnamed x10 -> x7, local copies, waits for them, and re-layouts: 18.5 us -> 4.42 us
    convert_element_type x2 -> x0, local copies, waits for them, and re-layouts: 8.03 us -> none  [the longest x1 4.02 us: body(): w_gate.astype(jnp.bfloat16)]
    convert_element_type x3 -> x0, other arithmetic: 5.28 us -> none  [the longest x1 3.23 us: body(): w_gate.astype(jnp.bfloat16)]
  transfers between devices with their start and end apart: 3 -> 0, of which waited for: 1 -> 0; matrix products, arithmetic and copies ran while one was open for 21% -> 0% of each run, Pallas kernels for 0% -> 0%
where the time goes in v1:
time: 89.3 us; the launch traced here: 88.5 us
  Pallas kernels  83.4 us (93%)
  local copies, waits for them, and re-layouts  4.42 us (5%)
    pallas_call x1, Pallas kernels, body(): pl.pallas_call(kernel, out_shape=(jax.ShapeDtypeStruct((experts, tiles, S...  83.4 us
    unnamed x7, local copies, waits for them, and re-layouts  4.42 us

profile of v1, /device:TPU:6, one launch (start us, length us, event | category | flops | bytes accessed | tf_op | source)
XLA Modules:
  0.0 88.5 jit_solution(56994679481707309)
XLA Ops:
  0.6 0.0 copy-start
  0.6 0.7 copy-done
  1.3 0.0 copy-start.1
  1.3 0.7 copy-done.1
  2.0 83.4 %serve.1 = (bf16[16,3,8,2048]{3,2,1,0:T(8,128)(2,1)S(1)}, bf16[16,3,8,2048]{3,2,1,0:T(8,128)(2,1)S(1)}, bf16[2048,128]{1,0:T(8,128)(2,1)S(1)}) custom-call(f32[8,128,768]{2,1,0:T(8,128)} %bitcast.10, f32[8,128,768]{2,1,0:T(8,128)} %bitcast.11, f32[16,64]{1,0:T(8,128)S(1)} %bitcast.8, f32[1,64]{1,0:T(1,128)S(1)} %bitcast.9), custom_call_target="tpu_custom_call" | custom-call | tf_op jit(solution)/shard_map/serve/pallas_call | solution.py:220
  85.4 1.1 %copy.10 = bf16[16,24,2048]{2,1,0:T(8,128)(2,1)} copy(bf16[16,24,2048]{2,1,0:T(8,128)(2,1)S(1)} %bitcast.7) | data formatting | bytes 3145728
  86.6 1.1 %copy.11 = bf16[16,24,2048]{2,1,0:T(8,128)(2,1)} copy(bf16[16,24,2048]{2,1,0:T(8,128)(2,1)S(1)} %bitcast.6) | data formatting | bytes 3145728
  87.7 0.8 copy.12
Async XLA Ops:
  0.6 0.7 copy-start
  1.3 0.7 copy-start.1

commit v2 on v1

--- a/solution.py
+++ b/solution.py
@@ -9,6 +9,8 @@
 NZ, NX, NY, CORES = 8, 4, 4, 2
 ROWS = NZ * NX
 LANES, SUB = 128, 8
+TOGETHER = 8
+PARTS = 4
 
 
 def place():
@@ -22,18 +24,17 @@
 
 def rows_of(k):
     _, _, z, x = place()
-    return beside(z, k // NX, NZ) * NX + beside(x, lax.rem(k, NX), NX)
+    return beside(z, lax.rem(k, NZ), NZ) * NX + beside(x, k // NZ, NX)
 
 
 def merged(even, odd):
     low = lax.broadcasted_iota(jnp.int32, even.shape, even.ndim - 1) < LANES // 2
-    turned_odd = pltpu.roll(odd, LANES // 2, odd.ndim - 1)
-    turned_even = pltpu.roll(even, LANES // 2, even.ndim - 1)
-    return jnp.where(low, even, turned_odd), jnp.where(low, turned_even, odd)
+    turned = pltpu.roll(jnp.where(low, odd, even), LANES // 2, even.ndim - 1)
+    return jnp.where(low, even, turned), jnp.where(low, turned, odd)
 
 
 def kernel(
-    gate, up, weight, gain, out_gate, out_up, out_router,
+    gate, up, weight, out_gate, out_up, out_router,
     staged, send, recv, pieces, in_sem, send_sem, recv_sem, piece_send, piece_recv,
 ):
     y, core, z, x = place()
@@ -65,7 +66,7 @@
     for peer in (*y_peers, partner):
         pl.semaphore_signal(barrier, inc=1, device_id={"owner": peer}, device_id_type=MESH)
 
-    scaled = weight[...] * gain[...]
+    scaled = weight[...]
     pieces[core, y, x, z] = jnp.concatenate([scaled[:SUB], scaled[SUB:]], axis=1).astype(jnp.bfloat16)
 
     def prepare(p):
@@ -99,20 +100,23 @@
         ).wait_recv()
 
     def assemble(p):
-        def pair(j, _):
-            for s in (2 * j, 2 * j + 1):
-                @pl.when(s != rows)
-                def _():
-                    arrived(p, s)
-
-            low, high = merged(recv[p, 2 * j], recv[p, 2 * j + 1])
-            lanes = pl.ds(pl.multiple_of(j * LANES, LANES), LANES)
-            for a, out in enumerate((out_gate, out_up)):
-                out[2 * p, :, :, lanes] = low[a * tiles : (a + 1) * tiles]
-                out[2 * p + 1, :, :, lanes] = high[a * tiles : (a + 1) * tiles]
+        def some(t, _):
+            for i in range(TOGETHER):
+                for s in (2 * (t * TOGETHER + i), 2 * (t * TOGETHER + i) + 1):
+                    @pl.when(s != rows)
+                    def _():
+                        arrived(p, s)
+
+            for i in range(TOGETHER):
+                j = t * TOGETHER + i
+                low, high = merged(recv[p, 2 * j], recv[p, 2 * j + 1])
+                lanes = pl.ds(pl.multiple_of(j * LANES, LANES), LANES)
+                for a, out in enumerate((out_gate, out_up)):
+                    out[2 * p, :, :, lanes] = low[a * tiles : (a + 1) * tiles]
+                    out[2 * p + 1, :, :, lanes] = high[a * tiles : (a + 1) * tiles]
             return 0
 
-        lax.fori_loop(0, ROWS // 2, pair, 0)
+        lax.fori_loop(0, ROWS // 2 // TOGETHER, some, 0)
 
     def to_z(k):
         mine = pieces.at[core, y, x, z]
@@ -211,6 +215,20 @@
     lax.fori_loop(0, pairs, sent, 0)
 
 
+def store(*refs):
+    count = len(refs) // 2
+    copies = []
+    for k, (source, target) in enumerate(zip(refs[:count], refs[count : 2 * count])):
+        step = source.shape[0] // PARTS
+        for i in range(PARTS):
+            part = pl.ds(i * step, step)
+            copies.append(pltpu.make_async_copy(source.at[part], target.at[part], refs[-1].at[k, i]))
+    for copy in copies:
+        copy.start()
+    for copy in copies:
+        copy.wait()
+
+
 def body(w_gate, w_up, router_weight, router_gain):
     experts, share, width = w_gate.shape
     pairs, model = experts // 2, share * ROWS
@@ -224,7 +242,7 @@
             jax.ShapeDtypeStruct((experts, tiles, SUB, model), jnp.bfloat16),
             jax.ShapeDtypeStruct((model, experts * NY * CORES), jnp.bfloat16),
         ),
-        in_specs=[anywhere, anywhere, vmem, vmem],
+        in_specs=[anywhere, anywhere, vmem],
         out_specs=(vmem, vmem, vmem),
         scratch_shapes=[
             pltpu.VMEM((pairs, 2, 2 * share, width), jnp.float32),
@@ -239,7 +257,16 @@
         ],
         compiler_params=pltpu.CompilerParams(collective_id=0, has_side_effects=True, vmem_limit_bytes=50000000),
         name="serve",
-    )(w_gate.reshape(paired), w_up.reshape(paired), router_weight.T, router_gain.reshape(1, share))
+    )(w_gate.reshape(paired), w_up.reshape(paired), (router_weight * router_gain[:, None]).T)
+    gate, up, router = pl.pallas_call(
+        store,
+        out_shape=tuple(jax.ShapeDtypeStruct(v.shape, v.dtype) for v in (gate, up, router)),
+        in_specs=[vmem] * 3,
+        out_specs=(anywhere,) * 3,
+        scratch_shapes=[pltpu.SemaphoreType.DMA((3, PARTS))],
+        compiler_params=pltpu.CompilerParams(vmem_limit_bytes=50000000),
+        name="store",
+    )(gate, up, router)
     shape = (experts, tiles * SUB, model)
     return gate.reshape(shape), up.reshape(shape), router
 

time: 89.3 us -> 86.4 us (0.968)
  local copies, waits for them, and re-layouts: 4.42 us -> 0 us
  Pallas kernels: 83.4 us -> 84.7 us
    unnamed x7 -> x0, local copies, waits for them, and re-layouts: 4.42 us -> none
    pallas_call x0 -> x1, Pallas kernels: none -> 1.93 us  [body(): pl.pallas_call(store, out_shape=tuple((jax.ShapeDtypeStruct(v.shape, v.dt...]
where the time goes in v2:
time: 86.4 us; the launch traced here: 86 us
  Pallas kernels  84.7 us (98%)
    pallas_call x1, Pallas kernels, body(): pl.pallas_call(kernel, out_shape=(jax.ShapeDtypeStruct((experts, tiles, S...  82.8 us
    pallas_call x1, Pallas kernels, body(): pl.pallas_call(store, out_shape=tuple((jax.ShapeDtypeStruct(v.shape, v.dt...  1.93 us

profile of v2, /device:TPU:6, one launch (start us, length us, event | category | flops | bytes accessed | tf_op | source)
XLA Modules:
  0.0 86.0 jit_solution(7194841004491226365)
XLA Ops:
  0.6 0.7 multiply_bitcast_fusion.weight
  1.3 82.8 %serve.1 = (bf16[16,3,8,2048]{3,2,1,0:T(8,128)(2,1)S(1)}, bf16[16,3,8,2048]{3,2,1,0:T(8,128)(2,1)S(1)}, bf16[2048,128]{1,0:T(8,128)(2,1)S(1)}) custom-call(f32[8,128,768]{2,1,0:T(8,128)} %bitcast.6, f32[8,128,768]{2,1,0:T(8,128)} %bitcast.7, f32[16,64]{1,0:T(8,128)S(1)} %multiply_bitcast_fusion.weight), custom_call_target="tpu_custom_call" | custom-call | tf_op jit(solution)/shard_map/serve/pallas_call | solution.py:238
  84.1 1.9 %store.1 = (bf16[16,3,8,2048]{3,2,1,0:T(8,128)(2,1)}, bf16[16,3,8,2048]{3,2,1,0:T(8,128)(2,1)}, bf16[2048,128]{1,0:T(8,128)(2,1)}) custom-call(bf16[16,3,8,2048]{3,2,1,0:T(8,128)(2,1)S(1)} %get-tuple-element.9.refs_0_, bf16[16,3,8,2048]{3,2,1,0:T(8,128)(2,1)S(1)} %get-tuple-element.10.refs_1_, bf16[2048,128]{1,0:T(8,128)(2,1)S(1)} %get-tuple-element.11.refs_2_), custom_call_target="tpu_custom_call" | custom-call | tf_op jit(solution)/shard_map/store/pallas_call | solution.py:261

commit v3 on v2

--- a/solution.py
+++ b/solution.py
@@ -11,20 +11,16 @@
 LANES, SUB = 128, 8
 TOGETHER = 8
 PARTS = 4
+ORDER = [(dx, dz) for dx in (2, 1, 3, 0) for dz in (4, 3, 5, 2, 6, 1, 7, 0) if dx or dz]
 
 
 def place():
     owner, rows = lax.axis_index("owner"), lax.axis_index("rows")
-    return owner // CORES, lax.rem(owner, CORES), rows // NX, lax.rem(rows, NX)
+    return owner // CORES, owner % CORES, rows // NX, rows % NX
 
 
 def beside(value, step, count):
-    return lax.rem(value + step, count)
-
-
-def rows_of(k):
-    _, _, z, x = place()
-    return beside(z, lax.rem(k, NZ), NZ) * NX + beside(x, k // NZ, NX)
+    return (value + step) % count
 
 
 def merged(even, odd):
@@ -45,7 +41,7 @@
     sources = (gate, up)
 
     def load(a, p):
-        return pltpu.make_async_copy(sources[a].at[p], staged.at[p, a], in_sem.at[p, a])
+        return pltpu.make_async_copy(sources[a].at[p], staged.at[p, a], in_sem.at[p])
 
     def load_all(p, _):
         for a in range(2):
@@ -56,11 +52,11 @@
 
     barrier = pltpu.get_barrier_semaphore()
 
-    def greet(k, _):
-        pl.semaphore_signal(barrier, inc=1, device_id={"rows": rows_of(k)}, device_id_type=MESH)
-        return 0
-
-    lax.fori_loop(1, ROWS, greet, 0)
+    lines = [beside(z, dz, NZ) * NX for dz in range(NZ)]
+    columns = [beside(x, dx, NX) for dx in range(NX)]
+    peers = [lines[dz] + columns[dx] for dx, dz in ORDER]
+    for peer in peers:
+        pl.semaphore_signal(barrier, inc=1, device_id={"rows": peer}, device_id_type=MESH)
     y_peers = [beside(y, k, NY) * CORES + core for k in range(1, NY)]
     partner = y * CORES + (1 - core)
     for peer in (*y_peers, partner):
@@ -70,8 +66,8 @@
     pieces[core, y, x, z] = jnp.concatenate([scaled[:SUB], scaled[SUB:]], axis=1).astype(jnp.bfloat16)
 
     def prepare(p):
+        pltpu.make_async_copy(gate.at[pl.ds(0, 2)], staged.at[p], in_sem.at[p]).wait()
         for a in range(2):
-            load(a, p).wait()
             for k in range(width // LANES):
                 block = staged[p, a, :, k * LANES : (k + 1) * LANES].T.reshape(LANES // SUB, SUB, LANES)
                 block = block.astype(jnp.bfloat16)
@@ -82,31 +78,25 @@
 
     def move(p, peer):
         return pltpu.make_async_remote_copy(
-            send.at[p, peer], recv.at[p, rows], send_sem.at[p], recv_sem.at[p, rows],
+            send.at[p, peer], recv.at[p, rows], send_sem.at[p], recv_sem.at[p],
             device_id={"rows": peer}, device_id_type=MESH,
         )
 
     def send_all(p):
-        def one(k, _):
-            move(p, rows_of(k)).start()
-            return 0
-
-        lax.fori_loop(1, ROWS, one, 0)
-
-    def arrived(p, source):
-        pltpu.make_async_remote_copy(
-            send.at[p, source], recv.at[p, source], send_sem.at[p], recv_sem.at[p, source],
+        for peer in peers:
+            move(p, peer).start()
+
+    def all_of(p):
+        others = pl.ds(0, ROWS - 1)
+        return pltpu.make_async_remote_copy(
+            send.at[p, others], recv.at[p, others], send_sem.at[p], recv_sem.at[p],
             device_id={"rows": rows}, device_id_type=MESH,
-        ).wait_recv()
+        )
 
     def assemble(p):
+        all_of(p).wait_recv()
+
         def some(t, _):
-            for i in range(TOGETHER):
-                for s in (2 * (t * TOGETHER + i), 2 * (t * TOGETHER + i) + 1):
-                    @pl.when(s != rows)
-                    def _():
-                        arrived(p, s)
-
             for i in range(TOGETHER):
                 j = t * TOGETHER + i
                 low, high = merged(recv[p, 2 * j], recv[p, 2 * j + 1])
@@ -121,28 +111,28 @@
     def to_z(k):
         mine = pieces.at[core, y, x, z]
         return pltpu.make_async_remote_copy(
-            mine, mine, piece_send.at[0, k], piece_recv.at[0, k],
+            mine, mine, piece_send.at[0], piece_recv.at[0],
             device_id={"rows": beside(z, k, NZ) * NX + x}, device_id_type=MESH,
         )
 
     def to_x(k):
         mine = pieces.at[core, y, x]
         return pltpu.make_async_remote_copy(
-            mine, mine, piece_send.at[1, k], piece_recv.at[1, k],
+            mine, mine, piece_send.at[1], piece_recv.at[1],
             device_id={"rows": z * NX + beside(x, k, NX)}, device_id_type=MESH,
         )
 
     def to_y(k):
         mine = pieces.at[core, y]
         return pltpu.make_async_remote_copy(
-            mine, mine, piece_send.at[2, k], piece_recv.at[2, k],
+            mine, mine, piece_send.at[2], piece_recv.at[2],
             device_id={"owner": beside(y, k, NY) * CORES + core}, device_id_type=MESH,
         )
 
     def to_core(k):
         mine = pieces.at[core]
         return pltpu.make_async_remote_copy(
-            mine, mine, piece_send.at[3, k], piece_recv.at[3, k],
+            mine, mine, piece_send.at[3], piece_recv.at[3],
             device_id={"owner": partner}, device_id_type=MESH,
         )
 
@@ -154,9 +144,16 @@
             to(k).start()
 
     def end(stage):
-        to, count = stages[stage]
-        for k in range(1, count):
-            to(k).wait()
+        whole = (
+            pieces.at[core, y, x, pl.ds(0, NZ - 1)],
+            pieces.at[core, y, pl.ds(0, NX - 1)],
+            pieces.at[core, pl.ds(0, NY - 1)],
+            pieces.at[core],
+        )[stage]
+        pltpu.make_async_remote_copy(
+            whole, whole, piece_send.at[stage], piece_recv.at[stage],
+            device_id={"rows": rows}, device_id_type=MESH,
+        ).wait()
 
     def router():
         for zz in range(NZ):
@@ -205,11 +202,7 @@
     lax.fori_loop(2, pairs, finish, 0)
 
     def sent(p, _):
-        others = pl.ds(0, ROWS - 1)
-        pltpu.make_async_remote_copy(
-            send.at[p, others], recv.at[p, others], send_sem.at[p], recv_sem.at[p, 0],
-            device_id={"rows": rows}, device_id_type=MESH,
-        ).wait_send()
+        all_of(p).wait_send()
         return 0
 
     lax.fori_loop(0, pairs, sent, 0)
@@ -249,11 +242,11 @@
             pltpu.VMEM((pairs, ROWS, 2 * tiles, SUB, LANES), jnp.bfloat16),
             pltpu.VMEM((pairs, ROWS, 2 * tiles, SUB, LANES), jnp.bfloat16),
             pltpu.VMEM((CORES, NY, NX, NZ, SUB, LANES), jnp.bfloat16),
-            pltpu.SemaphoreType.DMA((pairs, 2)),
             pltpu.SemaphoreType.DMA((pairs,)),
-            pltpu.SemaphoreType.DMA((pairs, ROWS)),
-            pltpu.SemaphoreType.DMA((4, NZ)),
-            pltpu.SemaphoreType.DMA((4, NZ)),
+            pltpu.SemaphoreType.DMA((pairs,)),
+            pltpu.SemaphoreType.DMA((pairs,)),
+            pltpu.SemaphoreType.DMA((4,)),
+            pltpu.SemaphoreType.DMA((4,)),
         ],
         compiler_params=pltpu.CompilerParams(collective_id=0, has_side_effects=True, vmem_limit_bytes=50000000),
         name="serve",

time: 86.4 us -> 83 us (0.961)
  Pallas kernels: 84.7 us -> 80.4 us
    pallas_call x1, Pallas kernels: 82.8 us -> 78.5 us  [body(): pl.pallas_call(kernel, out_shape=(jax.ShapeDtypeStruct((experts, tiles, S...]
where the time goes in v3:
time: 83 us; the launch traced here: 81.8 us
  Pallas kernels  80.4 us (97%)
    pallas_call x1, Pallas kernels, body(): pl.pallas_call(kernel, out_shape=(jax.ShapeDtypeStruct((experts, tiles, S...  78.5 us
    pallas_call x1, Pallas kernels, body(): pl.pallas_call(store, out_shape=tuple((jax.ShapeDtypeStruct(v.shape, v.dt...  1.93 us

profile of v3, /device:TPU:6, one launch (start us, length us, event | category | flops | bytes accessed | tf_op | source)
XLA Modules:
  0.0 81.8 jit_solution(2052686106765570428)
XLA Ops:
  0.6 0.7 multiply_bitcast_fusion.weight
  1.3 78.5 %serve.1 = (bf16[16,3,8,2048]{3,2,1,0:T(8,128)(2,1)S(1)}, bf16[16,3,8,2048]{3,2,1,0:T(8,128)(2,1)S(1)}, bf16[2048,128]{1,0:T(8,128)(2,1)S(1)}) custom-call(f32[8,128,768]{2,1,0:T(8,128)} %bitcast.6, f32[8,128,768]{2,1,0:T(8,128)} %bitcast.7, f32[16,64]{1,0:T(8,128)S(1)} %multiply_bitcast_fusion.weight), custom_call_target="tpu_custom_call" | custom-call | tf_op jit(solution)/shard_map/serve/pallas_call | solution.py:231
  79.8 1.9 %store.1 = (bf16[16,3,8,2048]{3,2,1,0:T(8,128)(2,1)}, bf16[16,3,8,2048]{3,2,1,0:T(8,128)(2,1)}, bf16[2048,128]{1,0:T(8,128)(2,1)}) custom-call(bf16[16,3,8,2048]{3,2,1,0:T(8,128)(2,1)S(1)} %get-tuple-element.9.refs_0_, bf16[16,3,8,2048]{3,2,1,0:T(8,128)(2,1)S(1)} %get-tuple-element.10.refs_1_, bf16[2048,128]{1,0:T(8,128)(2,1)S(1)} %get-tuple-element.11.refs_2_), custom_call_target="tpu_custom_call" | custom-call | tf_op jit(solution)/shard_map/store/pallas_call | solution.py:254

commit v4 on v3

--- a/solution.py
+++ b/solution.py
@@ -11,6 +11,12 @@
 LANES, SUB = 128, 8
 TOGETHER = 8
 PARTS = 4
+EARLY = 2
+REACH = [
+    [(0, dz) for dz in sorted({r + 1, NZ - r - 1}) if r + 1 <= NZ // 2]
+    + [(dx, dz) for dz in sorted({r, (NZ - r) % NZ}) for dx in range(1, NX)]
+    for r in range(NZ // 2 + 1)
+]
 ORDER = [(dx, dz) for dx in (2, 1, 3, 0) for dz in (4, 3, 5, 2, 6, 1, 7, 0) if dx or dz]
 
 
@@ -30,8 +36,8 @@
 
 
 def kernel(
-    gate, up, weight, out_gate, out_up, out_router,
-    staged, send, recv, pieces, in_sem, send_sem, recv_sem, piece_send, piece_recv,
+    gate, up, weight, gain, out_gate, out_up, out_router,
+    staged, weights, gains, send, recv, pieces, in_sem, router_sem, send_sem, recv_sem, piece_send, piece_recv, rounds,
 ):
     y, core, z, x = place()
     owner, rows = lax.axis_index("owner"), lax.axis_index("rows")
@@ -48,21 +54,30 @@
             load(a, p).start()
         return 0
 
-    lax.fori_loop(0, pairs, load_all, 0)
-
     barrier = pltpu.get_barrier_semaphore()
 
     lines = [beside(z, dz, NZ) * NX for dz in range(NZ)]
     columns = [beside(x, dx, NX) for dx in range(NX)]
     peers = [lines[dz] + columns[dx] for dx, dz in ORDER]
-    for peer in peers:
-        pl.semaphore_signal(barrier, inc=1, device_id={"rows": peer}, device_id_type=MESH)
     y_peers = [beside(y, k, NY) * CORES + core for k in range(1, NY)]
     partner = y * CORES + (1 - core)
+    beside_z = [lines[1] + x, lines[NZ - 1] + x]
+    for peer in beside_z + [z * NX + columns[dx] for dx in range(1, NX)]:
+        pl.semaphore_signal(barrier, inc=1, device_id={"rows": peer}, device_id_type=MESH)
     for peer in (*y_peers, partner):
         pl.semaphore_signal(barrier, inc=1, device_id={"owner": peer}, device_id_type=MESH)
 
-    scaled = weight[...]
+    router_loads = (
+        pltpu.make_async_copy(weight, weights, router_sem.at[0]),
+        pltpu.make_async_copy(gain, gains, router_sem.at[1]),
+    )
+    for copy in router_loads:
+        copy.start()
+    lax.fori_loop(0, pairs, load_all, 0)
+
+    for copy in router_loads:
+        copy.wait()
+    scaled = weights[...] * gains[...]
     pieces[core, y, x, z] = jnp.concatenate([scaled[:SUB], scaled[SUB:]], axis=1).astype(jnp.bfloat16)
 
     def prepare(p):
@@ -169,14 +184,23 @@
                 out_router[at : at + LANES, :] = block.T.astype(jnp.bfloat16)
 
     prepare(0)
-    pl.semaphore_wait(barrier, ROWS - 1 + NY)
-    begin(0)
-    send_all(0)
-    prepare(1)
-    send_all(1)
+    pl.semaphore_wait(barrier, 2 + (NX - 1) + NY)
+    for r, reach in enumerate(REACH):
+        if r:
+            pl.semaphore_wait(rounds.at[r - 1], 2)
+        if r < len(REACH) - 1:
+            for peer in beside_z:
+                pl.semaphore_signal(rounds.at[r], inc=1, device_id={"rows": peer}, device_id_type=MESH)
+        if r == len(REACH) - 2:
+            begin(0)
+        for p in range(EARLY):
+            if r == 0 and p > 0:
+                prepare(p)
+            for dx, dz in reach:
+                move(p, lines[dz] + columns[dx]).start()
     end(0)
     begin(1)
-    for p in (2, 3):
+    for p in range(EARLY, 4):
         prepare(p)
         send_all(p)
     end(1)
@@ -222,11 +246,16 @@
         copy.wait()
 
 
+def pinned(value):
+    return pltpu.with_memory_space_constraint(value, pltpu.HBM)
+
+
 def body(w_gate, w_up, router_weight, router_gain):
     experts, share, width = w_gate.shape
     pairs, model = experts // 2, share * ROWS
     tiles = width // ROWS // SUB
     paired = (pairs, 2 * share, width)
+    hbm = pl.BlockSpec(memory_space=pltpu.HBM)
     vmem, anywhere = pl.BlockSpec(memory_space=pltpu.VMEM), pl.BlockSpec(memory_space=pl.ANY)
     gate, up, router = pl.pallas_call(
         kernel,
@@ -235,22 +264,26 @@
             jax.ShapeDtypeStruct((experts, tiles, SUB, model), jnp.bfloat16),
             jax.ShapeDtypeStruct((model, experts * NY * CORES), jnp.bfloat16),
         ),
-        in_specs=[anywhere, anywhere, vmem],
+        in_specs=[anywhere, anywhere, hbm, hbm],
         out_specs=(vmem, vmem, vmem),
         scratch_shapes=[
             pltpu.VMEM((pairs, 2, 2 * share, width), jnp.float32),
+            pltpu.VMEM((experts, share), jnp.float32),
+            pltpu.VMEM((1, share), jnp.float32),
             pltpu.VMEM((pairs, ROWS, 2 * tiles, SUB, LANES), jnp.bfloat16),
             pltpu.VMEM((pairs, ROWS, 2 * tiles, SUB, LANES), jnp.bfloat16),
             pltpu.VMEM((CORES, NY, NX, NZ, SUB, LANES), jnp.bfloat16),
             pltpu.SemaphoreType.DMA((pairs,)),
+            pltpu.SemaphoreType.DMA((2,)),
             pltpu.SemaphoreType.DMA((pairs,)),
             pltpu.SemaphoreType.DMA((pairs,)),
             pltpu.SemaphoreType.DMA((4,)),
             pltpu.SemaphoreType.DMA((4,)),
+            pltpu.SemaphoreType.REGULAR((len(REACH) - 1,)),
         ],
         compiler_params=pltpu.CompilerParams(collective_id=0, has_side_effects=True, vmem_limit_bytes=50000000),
         name="serve",
-    )(w_gate.reshape(paired), w_up.reshape(paired), (router_weight * router_gain[:, None]).T)
+    )(w_gate.reshape(paired), w_up.reshape(paired), pinned(router_weight.T), pinned(router_gain.reshape(1, share)))
     gate, up, router = pl.pallas_call(
         store,
         out_shape=tuple(jax.ShapeDtypeStruct(v.shape, v.dtype) for v in (gate, up, router)),

time: 83 us -> 81.5 us (0.982); the launches traced: 81.8 us -> 81.4 us
  no operation moved by 1% of the time
where the time goes in v4:
time: 81.5 us; the launch traced here: 81.4 us
  Pallas kernels  80.7 us (99%)
    pallas_call x1, Pallas kernels, body(): pl.pallas_call(kernel, out_shape=(jax.ShapeDtypeStruct((experts, tiles, S...  78.8 us
    pallas_call x1, Pallas kernels, body(): pl.pallas_call(store, out_shape=tuple((jax.ShapeDtypeStruct(v.shape, v.dt...  1.93 us

profile of v4, /device:TPU:6, one launch (start us, length us, event | category | flops | bytes accessed | tf_op | source)
XLA Modules:
  0.0 81.4 jit_solution(16769538166151770452)
XLA Ops:
  0.6 78.8 %serve.1 = (bf16[16,3,8,2048]{3,2,1,0:T(8,128)(2,1)S(1)}, bf16[16,3,8,2048]{3,2,1,0:T(8,128)(2,1)S(1)}, bf16[2048,128]{1,0:T(8,128)(2,1)S(1)}) custom-call(f32[8,128,768]{2,1,0:T(8,128)} %bitcast.6, f32[8,128,768]{2,1,0:T(8,128)} %bitcast.7, f32[16,64]{1,0:T(8,128)} %bitcast.8, f32[1,64]{1,0:T(1,128)} %bitcast.9), custom_call_target="tpu_custom_call" | custom-call | tf_op jit(solution)/shard_map/serve/pallas_call | solution.py:260
  79.4 1.9 %store.1 = (bf16[16,3,8,2048]{3,2,1,0:T(8,128)(2,1)}, bf16[16,3,8,2048]{3,2,1,0:T(8,128)(2,1)}, bf16[2048,128]{1,0:T(8,128)(2,1)}) custom-call(bf16[16,3,8,2048]{3,2,1,0:T(8,128)(2,1)S(1)} %get-tuple-element.9.refs_0_, bf16[16,3,8,2048]{3,2,1,0:T(8,128)(2,1)S(1)} %get-tuple-element.10.refs_1_, bf16[2048,128]{1,0:T(8,128)(2,1)S(1)} %get-tuple-element.11.refs_2_), custom_call_target="tpu_custom_call" | custom-call | tf_op jit(solution)/shard_map/store/pallas_call | solution.py:287

commit v5 on v4

--- a/solution.py
+++ b/solution.py
@@ -12,6 +12,8 @@
 TOGETHER = 8
 PARTS = 4
 EARLY = 2
+LATE = 2
+GROUPS = ((0, 1, 2, 3), (4, 7, 5, 6))
 REACH = [
     [(0, dz) for dz in sorted({r + 1, NZ - r - 1}) if r + 1 <= NZ // 2]
     + [(dx, dz) for dz in sorted({r, (NZ - r) % NZ}) for dx in range(1, NX)]
@@ -93,7 +95,7 @@
 
     def move(p, peer):
         return pltpu.make_async_remote_copy(
-            send.at[p, peer], recv.at[p, rows], send_sem.at[p], recv_sem.at[p],
+            send.at[p, peer], recv.at[p, rows], send_sem.at[0], recv_sem.at[p],
             device_id={"rows": peer}, device_id_type=MESH,
         )
 
@@ -104,7 +106,7 @@
     def all_of(p):
         others = pl.ds(0, ROWS - 1)
         return pltpu.make_async_remote_copy(
-            send.at[p, others], recv.at[p, others], send_sem.at[p], recv_sem.at[p],
+            send.at[p, others], recv.at[p, others], send_sem.at[0], recv_sem.at[p],
             device_id={"rows": rows}, device_id_type=MESH,
         )
 
@@ -211,7 +213,18 @@
         send_all(p)
         return 0
 
-    lax.fori_loop(4, pairs, rest, 0)
+    lax.fori_loop(4, pairs - LATE, rest, 0)
+    for p in range(pairs - LATE, pairs):
+        prepare(p)
+    for group in GROUPS:
+        for column in columns[2], columns[1], columns[3], x:
+            for line in group:
+                for p in range(pairs - LATE, pairs):
+
+                    @pl.when(line * NX + column != rows)
+                    def _():
+                        move(p, line * NX + column).start()
+
     assemble(0)
     end(2)
     begin(3)
@@ -225,11 +238,11 @@
 
     lax.fori_loop(2, pairs, finish, 0)
 
-    def sent(p, _):
-        all_of(p).wait_send()
-        return 0
-
-    lax.fori_loop(0, pairs, sent, 0)
+    others = pl.ds(0, ROWS - 1)
+    pltpu.make_async_remote_copy(
+        send.at[:, others], recv.at[:, others], send_sem.at[0], recv_sem.at[0],
+        device_id={"rows": rows}, device_id_type=MESH,
+    ).wait_send()
 
 
 def store(*refs):
@@ -239,11 +252,11 @@
         step = source.shape[0] // PARTS
         for i in range(PARTS):
             part = pl.ds(i * step, step)
-            copies.append(pltpu.make_async_copy(source.at[part], target.at[part], refs[-1].at[k, i]))
+            copies.append(pltpu.make_async_copy(source.at[part], target.at[part], refs[-1].at[k]))
     for copy in copies:
         copy.start()
-    for copy in copies:
-        copy.wait()
+    for k, (source, target) in enumerate(zip(refs[:count], refs[count : 2 * count])):
+        pltpu.make_async_copy(source, target, refs[-1].at[k]).wait()
 
 
 def pinned(value):
@@ -275,7 +288,7 @@
             pltpu.VMEM((CORES, NY, NX, NZ, SUB, LANES), jnp.bfloat16),
             pltpu.SemaphoreType.DMA((pairs,)),
             pltpu.SemaphoreType.DMA((2,)),
-            pltpu.SemaphoreType.DMA((pairs,)),
+            pltpu.SemaphoreType.DMA((1,)),
             pltpu.SemaphoreType.DMA((pairs,)),
             pltpu.SemaphoreType.DMA((4,)),
             pltpu.SemaphoreType.DMA((4,)),
@@ -289,7 +302,7 @@
         out_shape=tuple(jax.ShapeDtypeStruct(v.shape, v.dtype) for v in (gate, up, router)),
         in_specs=[vmem] * 3,
         out_specs=(anywhere,) * 3,
-        scratch_shapes=[pltpu.SemaphoreType.DMA((3, PARTS))],
+        scratch_shapes=[pltpu.SemaphoreType.DMA((3,))],
         compiler_params=pltpu.CompilerParams(vmem_limit_bytes=50000000),
         name="store",
     )(gate, up, router)

time: 81.5 us -> 80.7 us (level)
  Pallas kernels: 80.7 us -> 79.8 us
where the time goes in v5:
time: 80.7 us; the launch traced here: 80.5 us
  Pallas kernels  79.8 us (99%)
    pallas_call x1, Pallas kernels, body(): pl.pallas_call(kernel, out_shape=(jax.ShapeDtypeStruct((experts, tiles, S...  78 us
    pallas_call x1, Pallas kernels, body(): pl.pallas_call(store, out_shape=tuple((jax.ShapeDtypeStruct(v.shape, v.dt...  1.85 us

profile of v5, /device:TPU:6, one launch (start us, length us, event | category | flops | bytes accessed | tf_op | source)
XLA Modules:
  0.0 80.5 jit_solution(17505416090693539335)
XLA Ops:
  0.6 78.0 %serve.1 = (bf16[16,3,8,2048]{3,2,1,0:T(8,128)(2,1)S(1)}, bf16[16,3,8,2048]{3,2,1,0:T(8,128)(2,1)S(1)}, bf16[2048,128]{1,0:T(8,128)(2,1)S(1)}) custom-call(f32[8,128,768]{2,1,0:T(8,128)} %bitcast.6, f32[8,128,768]{2,1,0:T(8,128)} %bitcast.7, f32[16,64]{1,0:T(8,128)} %bitcast.8, f32[1,64]{1,0:T(1,128)} %bitcast.9), custom_call_target="tpu_custom_call" | custom-call | tf_op jit(solution)/shard_map/serve/pallas_call | solution.py:273
  78.6 1.8 %store.1 = (bf16[16,3,8,2048]{3,2,1,0:T(8,128)(2,1)}, bf16[16,3,8,2048]{3,2,1,0:T(8,128)(2,1)}, bf16[2048,128]{1,0:T(8,128)(2,1)}) custom-call(bf16[16,3,8,2048]{3,2,1,0:T(8,128)(2,1)S(1)} %get-tuple-element.9.refs_0_, bf16[16,3,8,2048]{3,2,1,0:T(8,128)(2,1)S(1)} %get-tuple-element.10.refs_1_, bf16[2048,128]{1,0:T(8,128)(2,1)S(1)} %get-tuple-element.11.refs_2_), custom_call_target="tpu_custom_call" | custom-call | tf_op jit(solution)/shard_map/store/pallas_call | solution.py:300

commit v6 on v5

--- a/solution.py
+++ b/solution.py
@@ -9,11 +9,11 @@
 NZ, NX, NY, CORES = 8, 4, 4, 2
 ROWS = NZ * NX
 LANES, SUB = 128, 8
-TOGETHER = 8
+TOGETHER = 16
 PARTS = 4
 EARLY = 2
-LATE = 2
-GROUPS = ((0, 1, 2, 3), (4, 7, 5, 6))
+LATE = 4
+GROUPS = ((0, 1, 2, 3), (7, 4, 6, 5))
 REACH = [
     [(0, dz) for dz in sorted({r + 1, NZ - r - 1}) if r + 1 <= NZ // 2]
     + [(dx, dz) for dz in sorted({r, (NZ - r) % NZ}) for dx in range(1, NX)]
@@ -219,11 +219,12 @@
     for group in GROUPS:
         for column in columns[2], columns[1], columns[3], x:
             for line in group:
+                late = (line + NZ // 2 * core) % NZ * NX + column
                 for p in range(pairs - LATE, pairs):
 
-                    @pl.when(line * NX + column != rows)
+                    @pl.when(late != rows)
                     def _():
-                        move(p, line * NX + column).start()
+                        move(p, late).start()
 
     assemble(0)
     end(2)

time: 80.7 us -> 80.2 us (level)
  no operation moved by 1% of the time
where the time goes in v6:
time: 80.2 us; the launch traced here: 79.9 us
  Pallas kernels  79.2 us (99%)
    pallas_call x1, Pallas kernels, body(): pl.pallas_call(kernel, out_shape=(jax.ShapeDtypeStruct((experts, tiles, S...  77.4 us
    pallas_call x1, Pallas kernels, body(): pl.pallas_call(store, out_shape=tuple((jax.ShapeDtypeStruct(v.shape, v.dt...  1.85 us

profile of v6, /device:TPU:6, one launch (start us, length us, event | category | flops | bytes accessed | tf_op | source)
XLA Modules:
  0.0 79.9 jit_solution(6570153401341807295)
XLA Ops:
  0.6 77.4 %serve.1 = (bf16[16,3,8,2048]{3,2,1,0:T(8,128)(2,1)S(1)}, bf16[16,3,8,2048]{3,2,1,0:T(8,128)(2,1)S(1)}, bf16[2048,128]{1,0:T(8,128)(2,1)S(1)}) custom-call(f32[8,128,768]{2,1,0:T(8,128)} %bitcast.6, f32[8,128,768]{2,1,0:T(8,128)} %bitcast.7, f32[16,64]{1,0:T(8,128)} %bitcast.8, f32[1,64]{1,0:T(1,128)} %bitcast.9), custom_call_target="tpu_custom_call" | custom-call | tf_op jit(solution)/shard_map/serve/pallas_call | solution.py:274
  78.0 1.8 %store.1 = (bf16[16,3,8,2048]{3,2,1,0:T(8,128)(2,1)}, bf16[16,3,8,2048]{3,2,1,0:T(8,128)(2,1)}, bf16[2048,128]{1,0:T(8,128)(2,1)}) custom-call(bf16[16,3,8,2048]{3,2,1,0:T(8,128)(2,1)S(1)} %get-tuple-element.9.refs_0_, bf16[16,3,8,2048]{3,2,1,0:T(8,128)(2,1)S(1)} %get-tuple-element.10.refs_1_, bf16[2048,128]{1,0:T(8,128)(2,1)S(1)} %get-tuple-element.11.refs_2_), custom_call_target="tpu_custom_call" | custom-call | tf_op jit(solution)/shard_map/store/pallas_call | solution.py:301

commit v7 on v6

--- a/solution.py
+++ b/solution.py
@@ -12,7 +12,7 @@
 TOGETHER = 16
 PARTS = 4
 EARLY = 2
-LATE = 4
+LATE = 5
 GROUPS = ((0, 1, 2, 3), (7, 4, 6, 5))
 REACH = [
     [(0, dz) for dz in sorted({r + 1, NZ - r - 1}) if r + 1 <= NZ // 2]
@@ -202,7 +202,7 @@
                 move(p, lines[dz] + columns[dx]).start()
     end(0)
     begin(1)
-    for p in range(EARLY, 4):
+    for p in range(EARLY, pairs - LATE):
         prepare(p)
         send_all(p)
     end(1)
@@ -213,7 +213,7 @@
         send_all(p)
         return 0
 
-    lax.fori_loop(4, pairs - LATE, rest, 0)
+    lax.fori_loop(pairs - LATE, pairs - LATE, rest, 0)
     for p in range(pairs - LATE, pairs):
         prepare(p)
     for group in GROUPS:

time: 80.2 us -> 80.3 us (level)
  no operation moved by 1% of the time
where the time goes in v7:
time: 80.3 us; the launch traced here: 79.5 us
  Pallas kernels  78.9 us (98%)
    pallas_call x1, Pallas kernels, body(): pl.pallas_call(kernel, out_shape=(jax.ShapeDtypeStruct((experts, tiles, S...  77 us
    pallas_call x1, Pallas kernels, body(): pl.pallas_call(store, out_shape=tuple((jax.ShapeDtypeStruct(v.shape, v.dt...  1.85 us

profile of v7, /device:TPU:6, one launch (start us, length us, event | category | flops | bytes accessed | tf_op | source)
XLA Modules:
  0.0 79.5 jit_solution(11997173261571677292)
XLA Ops:
  0.6 77.0 %serve.1 = (bf16[16,3,8,2048]{3,2,1,0:T(8,128)(2,1)S(1)}, bf16[16,3,8,2048]{3,2,1,0:T(8,128)(2,1)S(1)}, bf16[2048,128]{1,0:T(8,128)(2,1)S(1)}) custom-call(f32[8,128,768]{2,1,0:T(8,128)} %bitcast.6, f32[8,128,768]{2,1,0:T(8,128)} %bitcast.7, f32[16,64]{1,0:T(8,128)} %bitcast.8, f32[1,64]{1,0:T(1,128)} %bitcast.9), custom_call_target="tpu_custom_call" | custom-call | tf_op jit(solution)/shard_map/serve/pallas_call | solution.py:274
  77.7 1.8 %store.1 = (bf16[16,3,8,2048]{3,2,1,0:T(8,128)(2,1)}, bf16[16,3,8,2048]{3,2,1,0:T(8,128)(2,1)}, bf16[2048,128]{1,0:T(8,128)(2,1)}) custom-call(bf16[16,3,8,2048]{3,2,1,0:T(8,128)(2,1)S(1)} %get-tuple-element.9.refs_0_, bf16[16,3,8,2048]{3,2,1,0:T(8,128)(2,1)S(1)} %get-tuple-element.10.refs_1_, bf16[2048,128]{1,0:T(8,128)(2,1)S(1)} %get-tuple-element.11.refs_2_), custom_call_target="tpu_custom_call" | custom-call | tf_op jit(solution)/shard_map/store/pallas_call | solution.py:301
